TPU v7x, 32 devices: a whole 2x2x4 slice. The times are simulated.
32 devices in a mesh: rows: 32 (over z, y, x, core).
Axes of the slice: x: 2, y: 2, z: 4, core: 2. Of those that a mesh axis runs over, the one named last changes fastest.
Arguments:
- adj_diag: int32 [512, 512], P('rows'), may hold values from -2147483648 to 2147483647
- adj_right: int32 [512, 512], P('rows'), may hold values from -2147483648 to 2147483647
- alive_diag: int32 [512, 512], P('rows'), may hold values from -2147483648 to 2147483647
- alive_right: int32 [512, 512], P('rows'), may hold values from -2147483648 to 2147483647
- truss_k: int32 [1], replicated, may hold values from 130 to 193
Outputs:
- support_field: float32 [16384, 1024], P('rows')
- removed_counts: int32 [3], replicated
All inputs are finite; a program needn't handle non-finite values.
Results may differ from a plain program's by a relative error of at most 0.0003.
Values may be sent and summed in bfloat16 or wider, within the bound.
A program may use at most 64 MiB of HBM per device.

v0:
```python
import functools

import jax
import jax.numpy as jnp
from jax import lax
from jax.experimental import pallas as pl
from jax.experimental.pallas import tpu as pltpu
from jax.sharding import PartitionSpec as P

F8 = jnp.float8_e4m3fn
F32 = jnp.float32
WORD = 32
ITERS = 3


def dot_nt(lhs, rhs):
    return lax.dot_general(lhs, rhs, (((1,), (1,)), ((), ())), preferred_element_type=F32)


def send(src, dst, send_sem, recv_sem, target):
    return pltpu.make_async_remote_copy(
        src_ref=src,
        dst_ref=dst,
        send_sem=send_sem,
        recv_sem=recv_sem,
        device_id=(target,),
        device_id_type=pl.DeviceIdType.MESH,
    )


def kernel(
    n, k_ref, ad_ref, ar_ref, ld_ref, lr_ref, out_ref, cnt_ref,
    k_smem, raw, own, halo, x, eye, tri, spare, psum_in, psum_next, psum_btw, mine, gathered,
    k_sem, raw_sems, send_sems, recv_sems, relay_sems, cnt_send, cnt_recv,
):
    t = ad_ref.shape[1]
    words = ad_ref.shape[0]
    me = lax.axis_index("rows")
    even = lax.rem(me, 2) == 0
    barrier = pltpu.get_barrier_semaphore()

    def greet(d, carry):
        pl.semaphore_signal(
            barrier, inc=1, device_id=(lax.rem(me + d, n),), device_id_type=pl.DeviceIdType.MESH
        )
        return carry

    for d in (1, n - 1, 2, n - 2):
        greet(d, 0)
    loads = [
        pltpu.make_async_copy(src, raw.at[i], raw_sems.at[i])
        for i, src in enumerate((ad_ref, ar_ref, ld_ref, lr_ref))
    ]
    for load in loads:
        load.start()
    k_load = pltpu.make_async_copy(k_ref, k_smem, k_sem)
    k_load.start()
    lax.fori_loop(3, n - 2, greet, 0)
    for load in loads:
        load.wait()
    own[0] = raw[0] & raw[2]
    own[1] = raw[1] & raw[3]

    AT, W, A = (pl.ds(i * t, t) for i in range(3))
    shift = lax.broadcasted_iota(jnp.int32, (WORD, t), 0)
    col = lax.broadcasted_iota(jnp.int32, (WORD, t), 1)

    half = t // 2

    def unpack(src, upper):
        for w in range(words):
            left = half if upper and 2 * w >= words else 0
            bits = (jnp.broadcast_to(src[w : w + 1, left:], (WORD, t - left)) >> shift[:, left:]) & 1
            if upper:
                bits = jnp.where(col[:, left:] - shift[:, left:] > WORD * w, bits, 0)
            yield pl.ds(WORD * w, WORD), pl.ds(left, t - left), bits.astype(F32).astype(F8)

    def put_across(src, j):
        for rows, _, bits in unpack(src, False):
            x[j, rows, A] = bits

    def put_transposed(j):
        x[j + 1, :, AT] = dot_nt(eye[...], x[j, :, A]).astype(F8)

    def put_within(src, j):
        for rows, cols, bits in unpack(src, True):
            tri[rows, cols] = bits
        flipped = dot_nt(eye[...], tri[...])
        x[j, :, W] = (flipped + tri[...].astype(F32)).astype(F8)

    row_id = lax.broadcasted_iota(jnp.int32, (t, t), 0)
    col_id = lax.broadcasted_iota(jnp.int32, (t, t), 1)
    eye[...] = jnp.where(row_id == col_id, 1.0, 0.0).astype(F32).astype(F8)
    tri[half:, :half] = jnp.zeros((t - half, half), F32).astype(F8)

    pl.semaphore_wait(barrier, n - 1)
    top, low = pl.ds(0, words // 2), pl.ds(words // 2, words // 2)
    whole, right = pl.ds(0, t), pl.ds(half, half)

    def pieces(source, slot, by, sends):
        parts = [(top, whole), (low, right if slot in (1, 3, 5) else whole)]
        return [
            send(
                source.at[rows, cols], halo.at[slot, rows, cols],
                sends.at[i], recv_sems.at[2 * slot + i], lax.rem(me + by + n, n),
            )
            for i, (rows, cols) in enumerate(parts)
        ]

    def start(slot):
        for piece in copies[slot]:
            piece.start()

    def arrive(slot):
        for piece in copies[slot]:
            piece.wait_recv()

    def left(copy):
        for piece in copy:
            piece.wait_send()

    routes = {2: (1, 1), 3: (0, -1), 1: (0, 1), 4: (1, -1), 0: (1, 2), 5: (0, -2)}
    copies = {
        slot: pieces(own.at[what], slot, by, send_sems.at[slot])
        for slot, (what, by) in routes.items()
    }
    to_right = pieces(halo.at[2], 0, 1, relay_sems)
    to_left = pieces(halo.at[3], 5, -1, relay_sems)
    start(3)
    start(2)

    @pl.when(even)
    def _():
        start(0)

    @pl.when(jnp.logical_not(even))
    def _():
        start(5)

    start(4)
    start(1)
    put_across(own.at[1], 1)

    k_load.wait()
    thresh = (k_smem[0] - 2).astype(F32)

    put_within(own.at[0], 1)
    put_transposed(1)
    psum_in[...] = dot_nt(x[1, :, t:], x[1, :, t:])
    psum_next[...] = dot_nt(x[2, :, AT], x[2, :, AT])
    psum_btw[...] = dot_nt(x[1, :, W], x[2, :, AT])

    def total(values):
        lanes = jnp.sum(values, axis=0, keepdims=True)
        return sum(lanes[:, i : i + 128] for i in range(0, t, 128))

    def keep(support, j, part):
        old = x[j, :, part].astype(F32)
        return old, jnp.where(support >= thresh, old, 0.0)

    def inside(j):
        return dot_nt(x[j], x[j])

    def between(j):
        return dot_nt(x[j, :, t:], x[j + 1, :, : 2 * t])

    def between_plain(j):
        return jnp.dot(x[j, :, A], x[j + 1, :, W], preferred_element_type=F32) + jnp.dot(
            x[j, :, W], x[j, :, A], preferred_element_type=F32
        )

    counts = []

    def own_count(old_w, new_w, old_a, new_a):
        counts.append(total((old_w - new_w) + 2.0 * (old_a - new_a)))

    arrive(2)

    @pl.when(even)
    def _():
        for piece in to_right:
            piece.start()

    put_across(halo.at[2], 0)
    put_transposed(0)
    old_w, w0 = keep(psum_in[...] + dot_nt(x[1, :, AT], x[1, :, AT]), 1, W)
    arrive(1)
    put_within(halo.at[1], 0)
    _, am = keep(between(0), 0, A)
    arrive(0)
    for rows, _, bits in unpack(halo.at[0], False):
        spare[rows, :] = bits
    x[0, :, AT] = dot_nt(eye[...], spare[...]).astype(F8)
    _, wm = keep(inside(0), 0, W)
    x[0, :, W] = wm.astype(F8)
    x[0, :, A] = am.astype(F8)
    x[1, :, W] = w0.astype(F8)
    put_transposed(0)
    arrive(3)

    @pl.when(jnp.logical_not(even))
    def _():
        for piece in to_left:
            piece.start()

    put_within(halo.at[3], 2)
    old_a, a0 = keep(psum_btw[...] + dot_nt(x[1, :, A], x[2, :, W]), 1, A)
    own_count(old_w, w0, old_a, a0)
    arrive(4)
    put_across(halo.at[4], 2)
    _, w1 = keep(psum_next[...] + dot_nt(x[2, :, t:], x[2, :, t:]), 2, W)
    arrive(5)
    put_within(halo.at[5], 3)
    _, a1 = keep(between_plain(2), 2, A)
    x[1, :, A] = a0.astype(F8)
    x[2, :, W] = w1.astype(F8)
    x[2, :, A] = a1.astype(F8)
    put_transposed(1)

    _, am = keep(between(0), 0, A)
    old_w, w0 = keep(inside(1), 1, W)
    old_a, a0 = keep(between(1), 1, A)
    own_count(old_w, w0, old_a, a0)
    _, w1 = keep(inside(2), 2, W)
    x[0, :, A] = am.astype(F8)
    x[1, :, W] = w0.astype(F8)
    x[1, :, A] = a0.astype(F8)
    x[2, :, W] = w1.astype(F8)
    put_transposed(0)

    support_w = inside(1)
    old_w, w0 = keep(support_w, 1, W)
    support_a = between_plain(1)
    old_a, a0 = keep(support_a, 1, A)
    own_count(old_w, w0, old_a, a0)
    lane = lax.broadcasted_iota(jnp.int32, (1, 128), 1)
    packed = jnp.zeros((1, 128), F32)
    for step, row in enumerate(counts):
        packed = jnp.where(lane == step, jnp.sum(row, axis=1, keepdims=True), packed)
    mine[...] = packed.astype(jnp.int32)

    def share(d, carry):
        send(mine, gathered.at[d - 1], cnt_send, cnt_recv, lax.rem(me + d, n)).start()
        return carry

    lax.fori_loop(1, n, share, 0)
    out_ref[:, :t] = support_w * w0
    out_ref[:, t:] = support_a * a0
    for slot in range(1, 5):
        left(copies[slot])

    @pl.when(even)
    def _():
        left(copies[0])
        left(to_right)

    @pl.when(jnp.logical_not(even))
    def _():
        left(copies[5])
        left(to_left)

    pltpu.make_async_copy(gathered, gathered, cnt_recv).wait()
    cnt_ref[: n - 1] = gathered[...]
    cnt_ref[n - 1] = mine[...]
    pltpu.make_async_copy(gathered, gathered, cnt_send).wait()


def finish(support_ref, cnt_ref, out_ref, removed_ref, sems):
    parts = sems.shape[0]
    rows = support_ref.shape[0] // parts
    copies = [
        pltpu.make_async_copy(
            support_ref.at[pl.ds(i * rows, rows)], out_ref.at[pl.ds(i * rows, rows)], sems.at[i]
        )
        for i in range(parts)
    ]
    for copy in copies:
        copy.start()
    summed = jnp.sum(cnt_ref[...], axis=0)
    lane = lax.broadcasted_iota(jnp.int32, summed.shape, 1)
    for step in range(removed_ref.shape[0]):
        removed_ref[step] = jnp.sum(jnp.where(lane == step, summed, 0)) // 2
    for copy in copies:
        copy.wait()


def on_device(n, adj_diag, adj_right, alive_diag, alive_right, truss_k):
    words, t = adj_diag.shape
    vmem = pl.BlockSpec(memory_space=pltpu.VMEM)
    smem = pl.BlockSpec(memory_space=pltpu.SMEM)
    hbm = pl.BlockSpec(memory_space=pltpu.HBM)
    args = [
        pltpu.with_memory_space_constraint(v, pltpu.HBM)
        for v in (adj_diag, adj_right, alive_diag, alive_right)
    ]
    support, counts = pl.pallas_call(
        functools.partial(kernel, n),
        out_shape=(
            jax.ShapeDtypeStruct((t, 2 * t), F32),
            jax.ShapeDtypeStruct((n, 1, 128), jnp.int32),
        ),
        in_specs=[hbm] * 5,
        out_specs=(vmem, vmem),
        scratch_shapes=[
            pltpu.SMEM((1,), jnp.int32),
            pltpu.VMEM((4, words, t), jnp.int32),
            pltpu.VMEM((2, words, t), jnp.int32),
            pltpu.VMEM((6, words, t), jnp.int32),
            pltpu.VMEM((4, t, 3 * t), F8),
            pltpu.VMEM((t, t), F8),
            pltpu.VMEM((t, t), F8),
            pltpu.VMEM((t, t), F8),
            pltpu.VMEM((t, t), F32),
            pltpu.VMEM((t, t), F32),
            pltpu.VMEM((t, t), F32),
            pltpu.VMEM((1, 128), jnp.int32),
            pltpu.VMEM((n - 1, 1, 128), jnp.int32),
            pltpu.SemaphoreType.DMA,
            pltpu.SemaphoreType.DMA((4,)),
            pltpu.SemaphoreType.DMA((6, 2)),
            pltpu.SemaphoreType.DMA((12,)),
            pltpu.SemaphoreType.DMA((2,)),
            pltpu.SemaphoreType.DMA,
            pltpu.SemaphoreType.DMA,
        ],
        compiler_params=pltpu.CompilerParams(collective_id=0, has_side_effects=True, vmem_limit_bytes=24 * 2**20),
    )(truss_k, *args)
    return pl.pallas_call(
        finish,
        out_shape=(
            jax.ShapeDtypeStruct((t, 2 * t), F32),
            jax.ShapeDtypeStruct((ITERS,), jnp.int32),
        ),
        in_specs=[vmem, vmem],
        out_specs=(hbm, smem),
        scratch_shapes=[pltpu.SemaphoreType.DMA((4,))],
        compiler_params=pltpu.CompilerParams(vmem_limit_bytes=2**20),
    )(support, counts)


def solution(mesh):
    row = P("rows", None)
    return jax.shard_map(
        functools.partial(on_device, mesh.shape["rows"]),
        mesh=mesh,
        in_specs=(row, row, row, row, P()),
        out_specs=(row, P()),
        check_vma=False,
    )
```

profile of v0, /device:TPU:0, one launch (start us, length us, event | category | flops | bytes accessed | tf_op | source)
XLA Modules:
  0.0 23.6 jit_solution(10623880856207365018)
XLA Ops:
  1.3 20.4 %shard_map.68 = (f32[512,1024]{1,0:T(8,128)S(1)}, s32[32,1,128]{2,1,0:T(1,128)S(1)}) custom-call(s32[1]{0:T(128)S(6)} %copy.7.k_ref, s32[16,512]{1,0:T(8,128)} %ad_ref.1, s32[16,512]{1,0:T(8,128)} %ar_ref.1, s32[16,512]{1,0:T(8,128)} %ld_ref.1, s32[16,512]{1,0:T(8,128)} %lr_ref.1), custom_call_target="tpu_custom_call" | custom-call | tf_op jit(solution)/shard_map/pallas_call | solution.py:296
  21.7 1.9 %shard_map.69 = (f32[512,1024]{1,0:T(8,128)}, s32[3]{0:T(128)}) custom-call(f32[512,1024]{1,0:T(8,128)S(1)} %get-tuple-element.4.support_ref, s32[32,1,128]{2,1,0:T(1,128)S(1)} %get-tuple-element.5.cnt_ref), custom_call_target="tpu_custom_call" | custom-call | tf_op jit(solution)/shard_map/pallas_call | solution.py:328
where the time goes:
time: 23.8 us; the launch traced here: 23.6 us
  Pallas kernels  22.3 us (94%)
  between operations  1.29 us (5%)
    pallas_call x1, Pallas kernels, on_device(): pl.pallas_call(functools.partial(kernel, n), out_shape=(jax.ShapeDtypeStr...  20.4 us
    pallas_call x1, Pallas kernels, on_device(): pl.pallas_call(finish, out_shape=(jax.ShapeDtypeStruct((t, 2 * t), F32),...  1.87 us

commit v1 on v0

--- a/solution.py
+++ b/solution.py
@@ -30,8 +30,9 @@
 
 def kernel(
     n, k_ref, ad_ref, ar_ref, ld_ref, lr_ref, out_ref, cnt_ref,
-    k_smem, raw, own, halo, x, eye, tri, spare, psum_in, psum_next, psum_btw, mine, gathered,
-    k_sem, raw_sems, send_sems, recv_sems, relay_sems, cnt_send, cnt_recv,
+    k_smem, raw, own, halo, hop, x, eye, tri, spare, psum_in, psum_next, psum_btw, psum_top, psum_far,
+    mine, gathered,
+    k_sem, raw_sems, send_sems, recv_sems, relay_sems, hop_send, hop_recv, cnt_send, cnt_recv, all_in,
 ):
     t = ad_ref.shape[1]
     words = ad_ref.shape[0]
@@ -39,14 +40,48 @@
     even = lax.rem(me, 2) == 0
     barrier = pltpu.get_barrier_semaphore()
 
-    def greet(d, carry):
+    odd = jnp.logical_not(even)
+    last, mid, mid_next, root = n - 1, n // 2, n // 2 + 1, n // 2 - 1
+
+    def greet(target):
         pl.semaphore_signal(
-            barrier, inc=1, device_id=(lax.rem(me + d, n),), device_id_type=pl.DeviceIdType.MESH
+            barrier, inc=1, device_id=(target,), device_id_type=pl.DeviceIdType.MESH
         )
-        return carry
-
-    for d in (1, n - 1, 2, n - 2):
-        greet(d, 0)
+
+    def at(by):
+        return lax.rem(me + by + n, n)
+
+    greet(at(-1))
+
+    @pl.when(me != last)
+    def _():
+        greet(at(1))
+
+    @pl.when(even)
+    def _():
+        greet(at(-2))
+
+    @pl.when(jnp.logical_and(odd, me != last))
+    def _():
+        greet(at(2))
+
+    @pl.when(me == last)
+    def _():
+        greet(mid)
+        greet(mid_next)
+
+    @pl.when(me == mid)
+    def _():
+        greet(1)
+
+    @pl.when(me == mid_next)
+    def _():
+        greet(0)
+
+    @pl.when(jnp.logical_or(me < root - 2, me > root + 1))
+    def _():
+        greet(root)
+
     loads = [
         pltpu.make_async_copy(src, raw.at[i], raw_sems.at[i])
         for i, src in enumerate((ad_ref, ar_ref, ld_ref, lr_ref))
@@ -55,7 +90,6 @@
         load.start()
     k_load = pltpu.make_async_copy(k_ref, k_smem, k_sem)
     k_load.start()
-    lax.fori_loop(3, n - 2, greet, 0)
     for load in loads:
         load.wait()
     own[0] = raw[0] & raw[2]
@@ -93,52 +127,97 @@
     eye[...] = jnp.where(row_id == col_id, 1.0, 0.0).astype(F32).astype(F8)
     tri[half:, :half] = jnp.zeros((t - half, half), F32).astype(F8)
 
-    pl.semaphore_wait(barrier, n - 1)
+    middle = jnp.logical_or(me == mid, me == mid_next)
+
+    @pl.when(middle)
+    def _():
+        pl.semaphore_wait(barrier, 4)
+
+    @pl.when(me == root)
+    def _():
+        pl.semaphore_wait(barrier, n - 1)
+
+    @pl.when(jnp.logical_not(jnp.logical_or(middle, me == root)))
+    def _():
+        pl.semaphore_wait(barrier, 3)
+
     top, low = pl.ds(0, words // 2), pl.ds(words // 2, words // 2)
     whole, right = pl.ds(0, t), pl.ds(half, half)
 
-    def pieces(source, slot, by, sends):
-        parts = [(top, whole), (low, right if slot in (1, 3, 5) else whole)]
+    def pieces(source, dest, upper, sends, recvs, target):
+        parts = [(top, whole), (low, right if upper else whole)]
         return [
             send(
-                source.at[rows, cols], halo.at[slot, rows, cols],
-                sends.at[i], recv_sems.at[2 * slot + i], lax.rem(me + by + n, n),
+                source.at[rows, cols], dest.at[rows, cols], sends.at[i], recvs[i], target
             )
             for i, (rows, cols) in enumerate(parts)
         ]
 
-    def start(slot):
-        for piece in copies[slot]:
+    def to_halo(source, slot, sends, target):
+        recvs = [recv_sems.at[2 * slot + i] for i in range(2)]
+        return pieces(source, halo.at[slot], slot in (1, 3, 5), sends, recvs, target)
+
+    def to_hop(what, place, slot, target):
+        recvs = [hop_recv.at[place, i] for i in range(2)]
+        return pieces(own.at[what], hop.at[place], slot in (3, 5), send_sems.at[slot], recvs, target)
+
+    def start(pieces):
+        for piece in pieces:
             piece.start()
 
-    def arrive(slot):
-        for piece in copies[slot]:
+    def arrive(pieces):
+        for piece in pieces:
             piece.wait_recv()
 
-    def left(copy):
-        for piece in copy:
+    def left(pieces):
+        for piece in pieces:
             piece.wait_send()
 
     routes = {2: (1, 1), 3: (0, -1), 1: (0, 1), 4: (1, -1), 0: (1, 2), 5: (0, -2)}
     copies = {
-        slot: pieces(own.at[what], slot, by, send_sems.at[slot])
+        slot: to_halo(own.at[what], slot, send_sems.at[slot], at(by))
         for slot, (what, by) in routes.items()
     }
-    to_right = pieces(halo.at[2], 0, 1, relay_sems)
-    to_left = pieces(halo.at[3], 5, -1, relay_sems)
-    start(3)
-    start(2)
+    to_right = to_halo(halo.at[2], 0, relay_sems, at(1))
+    to_left = to_halo(halo.at[3], 5, relay_sems, at(-1))
+    hop_in = {3: to_hop(0, 0, 3, mid_next), 4: to_hop(1, 1, 4, mid_next), 5: to_hop(0, 2, 5, mid)}
+    hop_out = {
+        slot: to_halo(hop.at[slot - 3], slot, hop_send.at[slot - 3], last) for slot in (3, 4, 5)
+    }
+
+    def start_or_hop(slot, source):
+        @pl.when(me == source)
+        def _():
+            start(hop_in[slot])
+
+        @pl.when(me != source)
+        def _():
+            start(copies[slot])
+
+    start_or_hop(3, 0)
+    start(copies[2])
 
     @pl.when(even)
     def _():
-        start(0)
-
-    @pl.when(jnp.logical_not(even))
-    def _():
-        start(5)
-
-    start(4)
-    start(1)
+        start(copies[0])
+
+    @pl.when(odd)
+    def _():
+        start_or_hop(5, 1)
+
+    start_or_hop(4, 0)
+    start(copies[1])
+
+    @pl.when(me == root)
+    def _():
+        def tell(d, carry):
+            pl.semaphore_signal(
+                all_in, inc=1, device_id=(at(d),), device_id_type=pl.DeviceIdType.MESH
+            )
+            return carry
+
+        lax.fori_loop(1, n, tell, 0)
+
     put_across(own.at[1], 1)
 
     k_load.wait()
@@ -164,30 +243,36 @@
     def between(j):
         return dot_nt(x[j, :, t:], x[j + 1, :, : 2 * t])
 
-    def between_plain(j):
-        return jnp.dot(x[j, :, A], x[j + 1, :, W], preferred_element_type=F32) + jnp.dot(
-            x[j, :, W], x[j, :, A], preferred_element_type=F32
-        )
-
     counts = []
 
     def own_count(old_w, new_w, old_a, new_a):
         counts.append(total((old_w - new_w) + 2.0 * (old_a - new_a)))
 
-    arrive(2)
+    arrive(copies[2])
 
     @pl.when(even)
     def _():
-        for piece in to_right:
-            piece.start()
+        start(to_right)
 
     put_across(halo.at[2], 0)
     put_transposed(0)
     old_w, w0 = keep(psum_in[...] + dot_nt(x[1, :, AT], x[1, :, AT]), 1, W)
-    arrive(1)
+    arrive(copies[1])
     put_within(halo.at[1], 0)
     _, am = keep(between(0), 0, A)
-    arrive(0)
+
+    @pl.when(me == mid_next)
+    def _():
+        for slot in (3, 4):
+            arrive(hop_in[slot])
+            start(hop_out[slot])
+
+    @pl.when(me == mid)
+    def _():
+        arrive(hop_in[5])
+        start(hop_out[5])
+
+    arrive(copies[0])
     for rows, _, bits in unpack(halo.at[0], False):
         spare[rows, :] = bits
     x[0, :, AT] = dot_nt(eye[...], spare[...]).astype(F8)
@@ -196,43 +281,49 @@
     x[0, :, A] = am.astype(F8)
     x[1, :, W] = w0.astype(F8)
     put_transposed(0)
-    arrive(3)
-
-    @pl.when(jnp.logical_not(even))
-    def _():
-        for piece in to_left:
-            piece.start()
+    _, am = keep(between(0), 0, A)
+    psum_in[...] = dot_nt(x[1, :, : 2 * t], x[1, :, : 2 * t])
+    x[0, :, A] = am.astype(F8)
+    put_transposed(0)
+    psum_top[...] = dot_nt(x[1, :, AT], x[1, :, AT])
+    arrive(copies[3])
+
+    @pl.when(odd)
+    def _():
+        start(to_left)
 
     put_within(halo.at[3], 2)
     old_a, a0 = keep(psum_btw[...] + dot_nt(x[1, :, A], x[2, :, W]), 1, A)
     own_count(old_w, w0, old_a, a0)
-    arrive(4)
+    arrive(copies[4])
     put_across(halo.at[4], 2)
     _, w1 = keep(psum_next[...] + dot_nt(x[2, :, t:], x[2, :, t:]), 2, W)
-    arrive(5)
-    put_within(halo.at[5], 3)
-    _, a1 = keep(between_plain(2), 2, A)
+    psum_far[...] = jnp.dot(x[2, :, W], x[2, :, A], preferred_element_type=F32)
     x[1, :, A] = a0.astype(F8)
     x[2, :, W] = w1.astype(F8)
-    x[2, :, A] = a1.astype(F8)
     put_transposed(1)
 
-    _, am = keep(between(0), 0, A)
-    old_w, w0 = keep(inside(1), 1, W)
+    old_w, w0 = keep(psum_in[...] + dot_nt(x[1, :, A], x[1, :, A]), 1, W)
     old_a, a0 = keep(between(1), 1, A)
     own_count(old_w, w0, old_a, a0)
-    _, w1 = keep(inside(2), 2, W)
-    x[0, :, A] = am.astype(F8)
+    psum_next[...] = dot_nt(x[2, :, : 2 * t], x[2, :, : 2 * t])
     x[1, :, W] = w0.astype(F8)
     x[1, :, A] = a0.astype(F8)
+
+    support_w = psum_top[...] + dot_nt(x[1, :, t:], x[1, :, t:])
+    old_w, w0 = keep(support_w, 1, W)
+    out_ref[:, :t] = support_w * w0
+    lost_w = total(old_w - w0)
+    psum_btw[...] = jnp.dot(x[1, :, W], x[1, :, A], preferred_element_type=F32)
+    arrive(copies[5])
+    put_within(halo.at[5], 3)
+    _, a1 = keep(psum_far[...] + dot_nt(x[2, :, A], x[3, :, W]), 2, A)
+    x[2, :, A] = a1.astype(F8)
+    _, w1 = keep(psum_next[...] + dot_nt(x[2, :, A], x[2, :, A]), 2, W)
     x[2, :, W] = w1.astype(F8)
-    put_transposed(0)
-
-    support_w = inside(1)
-    old_w, w0 = keep(support_w, 1, W)
-    support_a = between_plain(1)
+    support_a = psum_btw[...] + dot_nt(x[1, :, A], x[2, :, W])
     old_a, a0 = keep(support_a, 1, A)
-    own_count(old_w, w0, old_a, a0)
+    counts.append(lost_w + 2.0 * total(old_a - a0))
     lane = lax.broadcasted_iota(jnp.int32, (1, 128), 1)
     packed = jnp.zeros((1, 128), F32)
     for step, row in enumerate(counts):
@@ -243,8 +334,11 @@
         send(mine, gathered.at[d - 1], cnt_send, cnt_recv, lax.rem(me + d, n)).start()
         return carry
 
+    @pl.when(me != root)
+    def _():
+        pl.semaphore_wait(all_in, 1)
+
     lax.fori_loop(1, n, share, 0)
-    out_ref[:, :t] = support_w * w0
     out_ref[:, t:] = support_a * a0
     for slot in range(1, 5):
         left(copies[slot])
@@ -254,10 +348,19 @@
         left(copies[0])
         left(to_right)
 
-    @pl.when(jnp.logical_not(even))
+    @pl.when(odd)
     def _():
         left(copies[5])
         left(to_left)
+
+    @pl.when(me == mid_next)
+    def _():
+        left(hop_out[3])
+        left(hop_out[4])
+
+    @pl.when(me == mid)
+    def _():
+        left(hop_out[5])
 
     pltpu.make_async_copy(gathered, gathered, cnt_recv).wait()
     cnt_ref[: n - 1] = gathered[...]
@@ -306,10 +409,13 @@
             pltpu.VMEM((4, words, t), jnp.int32),
             pltpu.VMEM((2, words, t), jnp.int32),
             pltpu.VMEM((6, words, t), jnp.int32),
+            pltpu.VMEM((3, words, t), jnp.int32),
             pltpu.VMEM((4, t, 3 * t), F8),
             pltpu.VMEM((t, t), F8),
             pltpu.VMEM((t, t), F8),
             pltpu.VMEM((t, t), F8),
+            pltpu.VMEM((t, t), F32),
+            pltpu.VMEM((t, t), F32),
             pltpu.VMEM((t, t), F32),
             pltpu.VMEM((t, t), F32),
             pltpu.VMEM((t, t), F32),
@@ -320,8 +426,11 @@
             pltpu.SemaphoreType.DMA((6, 2)),
             pltpu.SemaphoreType.DMA((12,)),
             pltpu.SemaphoreType.DMA((2,)),
+            pltpu.SemaphoreType.DMA((3, 2)),
+            pltpu.SemaphoreType.DMA((3, 2)),
             pltpu.SemaphoreType.DMA,
             pltpu.SemaphoreType.DMA,
+            pltpu.SemaphoreType.REGULAR,
         ],
         compiler_params=pltpu.CompilerParams(collective_id=0, has_side_effects=True, vmem_limit_bytes=24 * 2**20),
     )(truss_k, *args)

time: 23.8 us -> 23.2 us (0.975)
  Pallas kernels: 22.3 us -> 21.8 us
    pallas_call x1, Pallas kernels: 20.4 us -> 19.9 us  [on_device(): pl.pallas_call(functools.partial(kernel, n), out_shape=(jax.ShapeDtypeStr...]
where the time goes in v1:
time: 23.2 us; the launch traced here: 23.1 us
  Pallas kernels  21.8 us (94%)
  between operations  1.29 us (6%)
    pallas_call x1, Pallas kernels, on_device(): pl.pallas_call(functools.partial(kernel, n), out_shape=(jax.ShapeDtypeStr...  19.9 us
    pallas_call x1, Pallas kernels, on_device(): pl.pallas_call(finish, out_shape=(jax.ShapeDtypeStruct((t, 2 * t), F32),...  1.87 us

profile of v1, /device:TPU:0, one launch (start us, length us, event | category | flops | bytes accessed | tf_op | source)
XLA Modules:
  0.0 23.1 jit_solution(925637908335598281)
XLA Ops:
  1.3 19.9 %shard_map.68 = (f32[512,1024]{1,0:T(8,128)S(1)}, s32[32,1,128]{2,1,0:T(1,128)S(1)}) custom-call(s32[1]{0:T(128)S(6)} %copy.7.k_ref, s32[16,512]{1,0:T(8,128)} %ad_ref.1, s32[16,512]{1,0:T(8,128)} %ar_ref.1, s32[16,512]{1,0:T(8,128)} %ld_ref.1, s32[16,512]{1,0:T(8,128)} %lr_ref.1), custom_call_target="tpu_custom_call" | custom-call | tf_op jit(solution)/shard_map/pallas_call | solution.py:399
  21.2 1.9 %shard_map.69 = (f32[512,1024]{1,0:T(8,128)}, s32[3]{0:T(128)}) custom-call(f32[512,1024]{1,0:T(8,128)S(1)} %get-tuple-element.4.support_ref, s32[32,1,128]{2,1,0:T(1,128)S(1)} %get-tuple-element.5.cnt_ref), custom_call_target="tpu_custom_call" | custom-call | tf_op jit(solution)/shard_map/pallas_call | solution.py:437

commit v2 on v1

--- a/solution.py
+++ b/solution.py
@@ -30,9 +30,10 @@
 
 def kernel(
     n, k_ref, ad_ref, ar_ref, ld_ref, lr_ref, out_ref, cnt_ref,
-    k_smem, raw, own, halo, hop, x, eye, tri, spare, psum_in, psum_next, psum_btw, psum_top, psum_far,
-    mine, gathered,
-    k_sem, raw_sems, send_sems, recv_sems, relay_sems, hop_send, hop_recv, cnt_send, cnt_recv, all_in,
+    k_smem, raw, own, halo, hop, x0, x1, x2, eye, tri, spare, sums, mine, gathered,
+    part_w0, part_a0, part_w1, part_a1, part_wm, part_sw, part_sa, part_top,
+    k_sem, raw_sems, send_sems, recv_sems, relay_sems, hop_send, hop_recv, cnt_send, cnt_recv,
+    all_in, last_in,
 ):
     t = ad_ref.shape[1]
     words = ad_ref.shape[0]
@@ -41,7 +42,7 @@
     barrier = pltpu.get_barrier_semaphore()
 
     odd = jnp.logical_not(even)
-    last, mid, mid_next, root = n - 1, n // 2, n // 2 + 1, n // 2 - 1
+    last, mid, mid_next, root = n - 1, n // 2, n // 2 + 1, n - 3
 
     def greet(target):
         pl.semaphore_signal(
@@ -65,20 +66,17 @@
     def _():
         greet(at(2))
 
-    @pl.when(me == last)
-    def _():
-        greet(mid)
-        greet(mid_next)
-
     @pl.when(me == mid)
     def _():
         greet(1)
+        greet(last)
 
     @pl.when(me == mid_next)
     def _():
         greet(0)
-
-    @pl.when(jnp.logical_or(me < root - 2, me > root + 1))
+        greet(last)
+
+    @pl.when(jnp.logical_or(me < root - 2, me == last))
     def _():
         greet(root)
 
@@ -90,6 +88,14 @@
         load.start()
     k_load = pltpu.make_async_copy(k_ref, k_smem, k_sem)
     k_load.start()
+    @pl.when(me == last)
+    def _():
+        pl.semaphore_wait(barrier, 5)
+        for target in (mid, mid_next):
+            pl.semaphore_signal(
+                last_in, inc=1, device_id=(target,), device_id_type=pl.DeviceIdType.MESH
+            )
+
     for load in loads:
         load.wait()
     own[0] = raw[0] & raw[2]
@@ -97,47 +103,55 @@
 
     AT, W, A = (pl.ds(i * t, t) for i in range(3))
     shift = lax.broadcasted_iota(jnp.int32, (WORD, t), 0)
-    col = lax.broadcasted_iota(jnp.int32, (WORD, t), 1)
+    slope = lax.broadcasted_iota(jnp.int32, (WORD, 128), 1) - shift[:, :128]
 
     half = t // 2
 
-    def unpack(src, upper):
+    def bits_of(src, w, cols):
+        span = cols.size
+        words32 = jnp.broadcast_to(src[w : w + 1, cols], (WORD, span))
+        return (words32 >> shift[:, :span]) & 1
+
+    def put_across(src, dst):
         for w in range(words):
-            left = half if upper and 2 * w >= words else 0
-            bits = (jnp.broadcast_to(src[w : w + 1, left:], (WORD, t - left)) >> shift[:, left:]) & 1
-            if upper:
-                bits = jnp.where(col[:, left:] - shift[:, left:] > WORD * w, bits, 0)
-            yield pl.ds(WORD * w, WORD), pl.ds(left, t - left), bits.astype(F32).astype(F8)
-
-    def put_across(src, j):
-        for rows, _, bits in unpack(src, False):
-            x[j, rows, A] = bits
-
-    def put_transposed(j):
-        x[j + 1, :, AT] = dot_nt(eye[...], x[j, :, A]).astype(F8)
-
-    def put_within(src, j):
-        for rows, cols, bits in unpack(src, True):
-            tri[rows, cols] = bits
-        flipped = dot_nt(eye[...], tri[...])
-        x[j, :, W] = (flipped + tri[...].astype(F32)).astype(F8)
-
-    row_id = lax.broadcasted_iota(jnp.int32, (t, t), 0)
-    col_id = lax.broadcasted_iota(jnp.int32, (t, t), 1)
+            dst[pl.ds(WORD * w, WORD), :] = bits_of(src, w, pl.ds(0, t)).astype(F32).astype(F8)
+
+    halves = (pl.ds(0, half), pl.ds(half, half))
+
+    def flipped(src, rows, cols):
+        return dot_nt(eye[...], src[cols, rows])
+
+    def put_flipped(src, dst):
+        for rows in halves:
+            for cols in halves:
+                dst[rows, cols] = flipped(src, rows, cols).astype(F8)
+
+    def put_within(src, dst):
+        for w in range(words):
+            rows, edge = pl.ds(WORD * w, WORD), WORD * w // 128 * 128
+            bits = bits_of(src, w, pl.ds(edge, 128))
+            bits = jnp.where(slope > WORD * w - edge, bits, 0)
+            tri[rows, pl.ds(edge, 128)] = bits.astype(F32).astype(F8)
+            if edge + 128 < t:
+                rest = pl.ds(edge + 128, t - edge - 128)
+                tri[rows, rest] = bits_of(src, w, rest).astype(F32).astype(F8)
+        for rows in halves:
+            both = flipped(tri, rows, rows) + tri[rows, rows].astype(F32)
+            dst[rows, rows] = both.astype(F8)
+        first, second = halves
+        dst[first, second] = tri[first, second]
+        dst[second, first] = flipped(tri, second, first).astype(F8)
+
+    row_id = lax.broadcasted_iota(jnp.int32, (half, half), 0)
+    col_id = lax.broadcasted_iota(jnp.int32, (half, half), 1)
     eye[...] = jnp.where(row_id == col_id, 1.0, 0.0).astype(F32).astype(F8)
-    tri[half:, :half] = jnp.zeros((t - half, half), F32).astype(F8)
-
-    middle = jnp.logical_or(me == mid, me == mid_next)
-
-    @pl.when(middle)
-    def _():
-        pl.semaphore_wait(barrier, 4)
+    tri[...] = jnp.zeros((t, t), F32).astype(F8)
 
     @pl.when(me == root)
     def _():
         pl.semaphore_wait(barrier, n - 1)
 
-    @pl.when(jnp.logical_not(jnp.logical_or(middle, me == root)))
+    @pl.when(jnp.logical_and(me != root, me != last))
     def _():
         pl.semaphore_wait(barrier, 3)
 
@@ -196,17 +210,12 @@
 
     start_or_hop(3, 0)
     start(copies[2])
-
-    @pl.when(even)
-    def _():
-        start(copies[0])
-
-    @pl.when(odd)
-    def _():
-        start_or_hop(5, 1)
-
     start_or_hop(4, 0)
     start(copies[1])
+
+    @pl.when(me == 1)
+    def _():
+        start(hop_in[5])
 
     @pl.when(me == root)
     def _():
@@ -218,112 +227,168 @@
 
         lax.fori_loop(1, n, tell, 0)
 
-    put_across(own.at[1], 1)
-
-    k_load.wait()
-    thresh = (k_smem[0] - 2).astype(F32)
-
-    put_within(own.at[0], 1)
-    put_transposed(1)
-    psum_in[...] = dot_nt(x[1, :, t:], x[1, :, t:])
-    psum_next[...] = dot_nt(x[2, :, AT], x[2, :, AT])
-    psum_btw[...] = dot_nt(x[1, :, W], x[2, :, AT])
-
     def total(values):
         lanes = jnp.sum(values, axis=0, keepdims=True)
         return sum(lanes[:, i : i + 128] for i in range(0, t, 128))
 
-    def keep(support, j, part):
-        old = x[j, :, part].astype(F32)
+    def keep(support, ref):
+        old = ref.astype(F32)
         return old, jnp.where(support >= thresh, old, 0.0)
 
-    def inside(j):
-        return dot_nt(x[j], x[j])
-
-    def between(j):
+    def put_sum(row, values):
+        sums[row : row + 1, :] = total(values)
+
+    def plain(lhs, rhs):
+        return jnp.dot(lhs, rhs, preferred_element_type=F32)
+
+    def square(block):
+        return dot_nt(block, block)
+
+    def between(x, j):
         return dot_nt(x[j, :, t:], x[j + 1, :, : 2 * t])
 
-    counts = []
-
-    def own_count(old_w, new_w, old_a, new_a):
-        counts.append(total((old_w - new_w) + 2.0 * (old_a - new_a)))
-
-    arrive(copies[2])
+    put_across(own.at[1], x0.at[1, :, A])
+    k_load.wait()
+    thresh = (k_smem[0] - 2).astype(F32)
+    put_within(own.at[0], x0.at[1, :, W])
+    put_flipped(x0.at[1, :, A], x0.at[2, :, AT])
+    part_w0[...] = square(x0[1, :, t:])
+    part_w1[...] = square(x0[2, :, AT])
+    part_a0[...] = dot_nt(x0[1, :, W], x0[2, :, AT])
 
     @pl.when(even)
     def _():
-        start(to_right)
-
-    put_across(halo.at[2], 0)
-    put_transposed(0)
-    old_w, w0 = keep(psum_in[...] + dot_nt(x[1, :, AT], x[1, :, AT]), 1, W)
-    arrive(copies[1])
-    put_within(halo.at[1], 0)
-    _, am = keep(between(0), 0, A)
+        start(copies[0])
+
+    @pl.when(jnp.logical_and(odd, me != 1))
+    def _():
+        start(copies[5])
+
+    def left_near():
+        arrive(copies[2])
+
+        @pl.when(even)
+        def _():
+            start(to_right)
+
+        arrive(copies[1])
+        put_across(halo.at[2], x0.at[0, :, A])
+        put_flipped(x0.at[0, :, A], x0.at[1, :, AT])
+        old, new = keep(part_w0[...] + square(x0[1, :, AT]), x0[1, :, W])
+        put_sum(0, old)
+        put_sum(2, new)
+        x1[1, :, W] = new.astype(F8)
+        put_within(halo.at[1], x0.at[0, :, W])
+        _, new = keep(between(x0, 0), x0[0, :, A])
+        x1[0, :, A] = new.astype(F8)
+        put_flipped(x1.at[0, :, A], x1.at[1, :, AT])
+        part_wm[...] = square(x0[0, :, t:])
+        part_w0[...] = square(x1[1, :, : 2 * t])
+
+    def left_far():
+        put_across(halo.at[0], spare)
+        put_flipped(spare, x0.at[0, :, AT])
+        _, new = keep(part_wm[...] + square(x0[0, :, AT]), x0[0, :, W])
+        x1[0, :, W] = new.astype(F8)
+        _, new = keep(between(x1, 0), x1[0, :, A])
+        spare[...] = new.astype(F8)
+        put_flipped(spare, x2.at[0, :, AT])
+        part_top[...] = square(x2[0, :, AT])
+
+    def right_near():
+        arrive(copies[3])
+
+        @pl.when(odd)
+        def _():
+            start(to_left)
+
+        arrive(copies[4])
+        put_within(halo.at[3], x0.at[2, :, W])
+        old, new = keep(part_a0[...] + dot_nt(x0[1, :, A], x0[2, :, W]), x0[1, :, A])
+        put_sum(1, old)
+        put_sum(3, new)
+        x1[1, :, A] = new.astype(F8)
+        put_flipped(x1.at[1, :, A], x1.at[2, :, AT])
+        put_across(halo.at[4], x0.at[2, :, A])
+        _, new = keep(part_w1[...] + square(x0[2, :, t:]), x0[2, :, W])
+        x1[2, :, W] = new.astype(F8)
+        part_a1[...] = plain(x0[2, :, W], x0[2, :, A])
+        part_w1[...] = square(x1[2, :, : 2 * t])
+
+    @pl.when(odd)
+    def _():
+        left_near()
+
+    @pl.when(even)
+    def _():
+        right_near()
+
+    @pl.when(me == mid)
+    def _():
+        pl.semaphore_wait(last_in, 1)
+        arrive(hop_in[5])
+        start(hop_out[5])
 
     @pl.when(me == mid_next)
     def _():
+        pl.semaphore_wait(last_in, 1)
         for slot in (3, 4):
             arrive(hop_in[slot])
             start(hop_out[slot])
 
-    @pl.when(me == mid)
-    def _():
-        arrive(hop_in[5])
-        start(hop_out[5])
-
-    arrive(copies[0])
-    for rows, _, bits in unpack(halo.at[0], False):
-        spare[rows, :] = bits
-    x[0, :, AT] = dot_nt(eye[...], spare[...]).astype(F8)
-    _, wm = keep(inside(0), 0, W)
-    x[0, :, W] = wm.astype(F8)
-    x[0, :, A] = am.astype(F8)
-    x[1, :, W] = w0.astype(F8)
-    put_transposed(0)
-    _, am = keep(between(0), 0, A)
-    psum_in[...] = dot_nt(x[1, :, : 2 * t], x[1, :, : 2 * t])
-    x[0, :, A] = am.astype(F8)
-    put_transposed(0)
-    psum_top[...] = dot_nt(x[1, :, AT], x[1, :, AT])
-    arrive(copies[3])
+    @pl.when(me == last)
+    def _():
+        arrive(copies[0])
+        left_far()
+
+    @pl.when(even)
+    def _():
+        left_near()
 
     @pl.when(odd)
     def _():
-        start(to_left)
-
-    put_within(halo.at[3], 2)
-    old_a, a0 = keep(psum_btw[...] + dot_nt(x[1, :, A], x[2, :, W]), 1, A)
-    own_count(old_w, w0, old_a, a0)
-    arrive(copies[4])
-    put_across(halo.at[4], 2)
-    _, w1 = keep(psum_next[...] + dot_nt(x[2, :, t:], x[2, :, t:]), 2, W)
-    psum_far[...] = jnp.dot(x[2, :, W], x[2, :, A], preferred_element_type=F32)
-    x[1, :, A] = a0.astype(F8)
-    x[2, :, W] = w1.astype(F8)
-    put_transposed(1)
-
-    old_w, w0 = keep(psum_in[...] + dot_nt(x[1, :, A], x[1, :, A]), 1, W)
-    old_a, a0 = keep(between(1), 1, A)
-    own_count(old_w, w0, old_a, a0)
-    psum_next[...] = dot_nt(x[2, :, : 2 * t], x[2, :, : 2 * t])
-    x[1, :, W] = w0.astype(F8)
-    x[1, :, A] = a0.astype(F8)
-
-    support_w = psum_top[...] + dot_nt(x[1, :, t:], x[1, :, t:])
-    old_w, w0 = keep(support_w, 1, W)
-    out_ref[:, :t] = support_w * w0
-    lost_w = total(old_w - w0)
-    psum_btw[...] = jnp.dot(x[1, :, W], x[1, :, A], preferred_element_type=F32)
-    arrive(copies[5])
-    put_within(halo.at[5], 3)
-    _, a1 = keep(psum_far[...] + dot_nt(x[2, :, A], x[3, :, W]), 2, A)
-    x[2, :, A] = a1.astype(F8)
-    _, w1 = keep(psum_next[...] + dot_nt(x[2, :, A], x[2, :, A]), 2, W)
-    x[2, :, W] = w1.astype(F8)
-    support_a = psum_btw[...] + dot_nt(x[1, :, A], x[2, :, W])
-    old_a, a0 = keep(support_a, 1, A)
-    counts.append(lost_w + 2.0 * total(old_a - a0))
+        right_near()
+
+    def finish_rounds(far):
+        arrive(copies[5])
+        put_within(halo.at[5], x0.at[3, :, W])
+        _, new = keep(part_w0[...] + square(x1[1, :, A]), x1[1, :, W])
+        put_sum(4, new)
+        x2[0, :, W] = new.astype(F8)
+        _, new = keep(between(x1, 1), x1[1, :, A])
+        put_sum(5, new)
+        x2[0, :, A] = new.astype(F8)
+        _, new = keep(part_a1[...] + dot_nt(x0[2, :, A], x0[3, :, W]), x0[2, :, A])
+        x1[2, :, A] = new.astype(F8)
+        part_sw[...] = square(x2[0, :, t:])
+        if far:
+            left_far()
+        _, new = keep(part_w1[...] + square(x1[2, :, A]), x1[2, :, W])
+        x2[1, :, W] = new.astype(F8)
+        part_sa[...] = plain(x2[0, :, W], x2[0, :, A])
+        support = part_sw[...] + part_top[...]
+        _, new = keep(support, x2[0, :, W])
+        put_sum(6, new)
+        out_ref[:, :t] = support * new
+        support = part_sa[...] + dot_nt(x2[0, :, A], x2[1, :, W])
+        _, new = keep(support, x2[0, :, A])
+        put_sum(7, new)
+        out_ref[:, t:] = support * new
+
+    @pl.when(me == last)
+    def _():
+        finish_rounds(False)
+
+    @pl.when(me != last)
+    def _():
+        arrive(copies[0])
+        finish_rounds(True)
+
+    counts = []
+    for step in range(ITERS):
+        before, after = sums[2 * step : 2 * step + 2, :], sums[2 * step + 2 : 2 * step + 4, :]
+        gone = before - after
+        counts.append(gone[0:1] + 2.0 * gone[1:2])
     lane = lax.broadcasted_iota(jnp.int32, (1, 128), 1)
     packed = jnp.zeros((1, 128), F32)
     for step, row in enumerate(counts):
@@ -339,7 +404,6 @@
         pl.semaphore_wait(all_in, 1)
 
     lax.fori_loop(1, n, share, 0)
-    out_ref[:, t:] = support_a * a0
     for slot in range(1, 5):
         left(copies[slot])
 
@@ -411,16 +475,15 @@
             pltpu.VMEM((6, words, t), jnp.int32),
             pltpu.VMEM((3, words, t), jnp.int32),
             pltpu.VMEM((4, t, 3 * t), F8),
+            pltpu.VMEM((3, t, 3 * t), F8),
+            pltpu.VMEM((2, t, 3 * t), F8),
+            pltpu.VMEM((t // 2, t // 2), F8),
             pltpu.VMEM((t, t), F8),
             pltpu.VMEM((t, t), F8),
-            pltpu.VMEM((t, t), F8),
-            pltpu.VMEM((t, t), F32),
-            pltpu.VMEM((t, t), F32),
-            pltpu.VMEM((t, t), F32),
-            pltpu.VMEM((t, t), F32),
-            pltpu.VMEM((t, t), F32),
+            pltpu.VMEM((8, 128), F32),
             pltpu.VMEM((1, 128), jnp.int32),
             pltpu.VMEM((n - 1, 1, 128), jnp.int32),
+            *[pltpu.VMEM((t, t), F32)] * 8,
             pltpu.SemaphoreType.DMA,
             pltpu.SemaphoreType.DMA((4,)),
             pltpu.SemaphoreType.DMA((6, 2)),
@@ -431,8 +494,9 @@
             pltpu.SemaphoreType.DMA,
             pltpu.SemaphoreType.DMA,
             pltpu.SemaphoreType.REGULAR,
+            pltpu.SemaphoreType.REGULAR,
         ],
-        compiler_params=pltpu.CompilerParams(collective_id=0, has_side_effects=True, vmem_limit_bytes=24 * 2**20),
+        compiler_params=pltpu.CompilerParams(collective_id=0, has_side_effects=True, vmem_limit_bytes=32 * 2**20),
     )(truss_k, *args)
     return pl.pallas_call(
         finish,

time: 23.2 us -> 22 us (0.948)
  Pallas kernels: 21.8 us -> 20.4 us
    pallas_call x1, Pallas kernels: 19.9 us -> 18.5 us  [on_device(): pl.pallas_call(functools.partial(kernel, n), out_shape=(jax.ShapeDtypeStr...]
where the time goes in v2:
time: 22 us; the launch traced here: 21.8 us
  Pallas kernels  20.4 us (93%)
  between operations  1.45 us (7%)
    pallas_call x1, Pallas kernels, on_device(): pl.pallas_call(functools.partial(kernel, n), out_shape=(jax.ShapeDtypeStr...  18.5 us
    pallas_call x1, Pallas kernels, on_device(): pl.pallas_call(finish, out_shape=(jax.ShapeDtypeStruct((t, 2 * t), F32),...  1.87 us

profile of v2, /device:TPU:0, one launch (start us, length us, event | category | flops | bytes accessed | tf_op | source)
XLA Modules:
  0.0 21.8 jit_solution(13256343337035092423)
XLA Ops:
  1.3 18.5 %shard_map.68 = (f32[512,1024]{1,0:T(8,128)S(1)}, s32[32,1,128]{2,1,0:T(1,128)S(1)}) custom-call(s32[1]{0:T(128)S(6)} %copy.7.k_ref, s32[16,512]{1,0:T(8,128)} %ad_ref.1, s32[16,512]{1,0:T(8,128)} %ar_ref.1, s32[16,512]{1,0:T(8,128)} %ld_ref.1, s32[16,512]{1,0:T(8,128)} %lr_ref.1), custom_call_target="tpu_custom_call" | custom-call | tf_op jit(solution)/shard_map/pallas_call | solution.py:463
  19.8 1.9 %shard_map.69 = (f32[512,1024]{1,0:T(8,128)}, s32[3]{0:T(128)}) custom-call(f32[512,1024]{1,0:T(8,128)S(1)} %get-tuple-element.4.support_ref, s32[32,1,128]{2,1,0:T(1,128)S(1)} %get-tuple-element.5.cnt_ref), custom_call_target="tpu_custom_call" | custom-call | tf_op jit(solution)/shard_map/pallas_call | solution.py:501

commit v3 on v2

--- a/solution.py
+++ b/solution.py
@@ -31,7 +31,7 @@
 def kernel(
     n, k_ref, ad_ref, ar_ref, ld_ref, lr_ref, out_ref, cnt_ref,
     k_smem, raw, own, halo, hop, x0, x1, x2, eye, tri, spare, sums, mine, gathered,
-    part_w0, part_a0, part_w1, part_a1, part_wm, part_sw, part_sa, part_top,
+    part_w0, part_a0, part_w1, part_top,
     k_sem, raw_sems, send_sems, recv_sems, relay_sems, hop_send, hop_recv, cnt_send, cnt_recv,
     all_in, last_in,
 ):
@@ -282,52 +282,36 @@
         _, new = keep(between(x0, 0), x0[0, :, A])
         x1[0, :, A] = new.astype(F8)
         put_flipped(x1.at[0, :, A], x1.at[1, :, AT])
-        part_wm[...] = square(x0[0, :, t:])
-        part_w0[...] = square(x1[1, :, : 2 * t])
 
     def left_far():
         put_across(halo.at[0], spare)
         put_flipped(spare, x0.at[0, :, AT])
-        _, new = keep(part_wm[...] + square(x0[0, :, AT]), x0[0, :, W])
+        _, new = keep(square(x0[0]), x0[0, :, W])
         x1[0, :, W] = new.astype(F8)
         _, new = keep(between(x1, 0), x1[0, :, A])
         spare[...] = new.astype(F8)
         put_flipped(spare, x2.at[0, :, AT])
-        part_top[...] = square(x2[0, :, AT])
-
-    def right_near():
+
+    def right_near(split):
         arrive(copies[3])
 
         @pl.when(odd)
         def _():
             start(to_left)
 
-        arrive(copies[4])
+        if not split:
+            arrive(copies[4])
         put_within(halo.at[3], x0.at[2, :, W])
         old, new = keep(part_a0[...] + dot_nt(x0[1, :, A], x0[2, :, W]), x0[1, :, A])
         put_sum(1, old)
         put_sum(3, new)
         x1[1, :, A] = new.astype(F8)
         put_flipped(x1.at[1, :, A], x1.at[2, :, AT])
+        if split:
+            arrive(copies[4])
         put_across(halo.at[4], x0.at[2, :, A])
         _, new = keep(part_w1[...] + square(x0[2, :, t:]), x0[2, :, W])
         x1[2, :, W] = new.astype(F8)
-        part_a1[...] = plain(x0[2, :, W], x0[2, :, A])
-        part_w1[...] = square(x1[2, :, : 2 * t])
-
-    @pl.when(odd)
-    def _():
-        left_near()
-
-    @pl.when(even)
-    def _():
-        right_near()
-
-    @pl.when(me == mid)
-    def _():
-        pl.semaphore_wait(last_in, 1)
-        arrive(hop_in[5])
-        start(hop_out[5])
 
     @pl.when(me == mid_next)
     def _():
@@ -336,53 +320,92 @@
             arrive(hop_in[slot])
             start(hop_out[slot])
 
+    @pl.when(odd)
+    def _():
+        left_near()
+
+    @pl.when(even)
+    def _():
+        right_near(False)
+
+    @pl.when(me == mid)
+    def _():
+        pl.semaphore_wait(last_in, 1)
+        arrive(hop_in[5])
+        start(hop_out[5])
+
     @pl.when(me == last)
     def _():
         arrive(copies[0])
         left_far()
+        part_w0[...] = square(x1[1, :, : 2 * t])
+        part_top[...] = square(x2[0, :, AT])
+        right_near(True)
 
     @pl.when(even)
     def _():
         left_near()
 
-    @pl.when(odd)
-    def _():
-        right_near()
-
-    def finish_rounds(far):
-        arrive(copies[5])
-        put_within(halo.at[5], x0.at[3, :, W])
-        _, new = keep(part_w0[...] + square(x1[1, :, A]), x1[1, :, W])
+    @pl.when(jnp.logical_and(odd, me != last))
+    def _():
+        right_near(False)
+
+    def finish_rounds(far, late):
+        if not late:
+            arrive(copies[5])
+            put_within(halo.at[5], x0.at[3, :, W])
+        inside = square(x1[1]) if far else part_w0[...] + square(x1[1, :, A])
+        _, new = keep(inside, x1[1, :, W])
         put_sum(4, new)
         x2[0, :, W] = new.astype(F8)
         _, new = keep(between(x1, 1), x1[1, :, A])
         put_sum(5, new)
         x2[0, :, A] = new.astype(F8)
-        _, new = keep(part_a1[...] + dot_nt(x0[2, :, A], x0[3, :, W]), x0[2, :, A])
-        x1[2, :, A] = new.astype(F8)
-        part_sw[...] = square(x2[0, :, t:])
+        first = plain(x0[2, :, W], x0[2, :, A])
+        if late:
+            part_a0[...] = first
+            part_w1[...] = square(x1[2, :, : 2 * t])
+        else:
+            _, new = keep(first + dot_nt(x0[2, :, A], x0[3, :, W]), x0[2, :, A])
+            x1[2, :, A] = new.astype(F8)
         if far:
             left_far()
-        _, new = keep(part_w1[...] + square(x1[2, :, A]), x1[2, :, W])
-        x2[1, :, W] = new.astype(F8)
-        part_sa[...] = plain(x2[0, :, W], x2[0, :, A])
-        support = part_sw[...] + part_top[...]
+        if not late:
+            _, new = keep(square(x1[2]), x1[2, :, W])
+            x2[1, :, W] = new.astype(F8)
+        support = square(x2[0]) if far else part_top[...] + square(x2[0, :, t:])
         _, new = keep(support, x2[0, :, W])
         put_sum(6, new)
         out_ref[:, :t] = support * new
-        support = part_sa[...] + dot_nt(x2[0, :, A], x2[1, :, W])
+        first = plain(x2[0, :, W], x2[0, :, A])
+        if late:
+            part_w0[...] = first
+            arrive(copies[5])
+            put_within(halo.at[5], x0.at[3, :, W])
+            support = part_a0[...] + dot_nt(x0[2, :, A], x0[3, :, W])
+            _, new = keep(support, x0[2, :, A])
+            x1[2, :, A] = new.astype(F8)
+            _, new = keep(part_w1[...] + square(x1[2, :, A]), x1[2, :, W])
+            x2[1, :, W] = new.astype(F8)
+            first = part_w0[...]
+        support = first + dot_nt(x2[0, :, A], x2[1, :, W])
         _, new = keep(support, x2[0, :, A])
         put_sum(7, new)
         out_ref[:, t:] = support * new
 
     @pl.when(me == last)
     def _():
-        finish_rounds(False)
-
-    @pl.when(me != last)
+        finish_rounds(False, False)
+
+    @pl.when(me == last - 1)
     def _():
         arrive(copies[0])
-        finish_rounds(True)
+        finish_rounds(True, True)
+
+    @pl.when(me < last - 1)
+    def _():
+        arrive(copies[0])
+        finish_rounds(True, False)
 
     counts = []
     for step in range(ITERS):
@@ -483,7 +506,7 @@
             pltpu.VMEM((8, 128), F32),
             pltpu.VMEM((1, 128), jnp.int32),
             pltpu.VMEM((n - 1, 1, 128), jnp.int32),
-            *[pltpu.VMEM((t, t), F32)] * 8,
+            *[pltpu.VMEM((t, t), F32)] * 4,
             pltpu.SemaphoreType.DMA,
             pltpu.SemaphoreType.DMA((4,)),
             pltpu.SemaphoreType.DMA((6, 2)),

time: 22 us -> 21.6 us (0.982)
  Pallas kernels: 20.4 us -> 19.9 us
    pallas_call x1, Pallas kernels: 18.5 us -> 18.1 us  [on_device(): pl.pallas_call(functools.partial(kernel, n), out_shape=(jax.ShapeDtypeStr...]
where the time goes in v3:
time: 21.6 us; the launch traced here: 21.4 us
  Pallas kernels  19.9 us (92%)
  between operations  1.45 us (7%)
    pallas_call x1, Pallas kernels, on_device(): pl.pallas_call(functools.partial(kernel, n), out_shape=(jax.ShapeDtypeStr...  18.1 us
    pallas_call x1, Pallas kernels, on_device(): pl.pallas_call(finish, out_shape=(jax.ShapeDtypeStruct((t, 2 * t), F32),...  1.87 us

profile of v3, /device:TPU:0, one launch (start us, length us, event | category | flops | bytes accessed | tf_op | source)
XLA Modules:
  0.0 21.4 jit_solution(17342791964184064389)
XLA Ops:
  1.3 18.1 %shard_map.68 = (f32[512,1024]{1,0:T(8,128)S(1)}, s32[32,1,128]{2,1,0:T(1,128)S(1)}) custom-call(s32[1]{0:T(128)S(6)} %copy.7.k_ref, s32[16,512]{1,0:T(8,128)} %ad_ref.1, s32[16,512]{1,0:T(8,128)} %ar_ref.1, s32[16,512]{1,0:T(8,128)} %ld_ref.1, s32[16,512]{1,0:T(8,128)} %lr_ref.1), custom_call_target="tpu_custom_call" | custom-call | tf_op jit(solution)/shard_map/pallas_call | solution.py:486
  19.3 1.9 %shard_map.69 = (f32[512,1024]{1,0:T(8,128)}, s32[3]{0:T(128)}) custom-call(f32[512,1024]{1,0:T(8,128)S(1)} %get-tuple-element.4.support_ref, s32[32,1,128]{2,1,0:T(1,128)S(1)} %get-tuple-element.5.cnt_ref), custom_call_target="tpu_custom_call" | custom-call | tf_op jit(solution)/shard_map/pallas_call | solution.py:524

commit v4 on v3

--- a/solution.py
+++ b/solution.py
@@ -33,7 +33,7 @@
     k_smem, raw, own, halo, hop, x0, x1, x2, eye, tri, spare, sums, mine, gathered,
     part_w0, part_a0, part_w1, part_top,
     k_sem, raw_sems, send_sems, recv_sems, relay_sems, hop_send, hop_recv, cnt_send, cnt_recv,
-    all_in, last_in,
+    all_in, last_in, near_in,
 ):
     t = ad_ref.shape[1]
     words = ad_ref.shape[0]
@@ -42,7 +42,7 @@
     barrier = pltpu.get_barrier_semaphore()
 
     odd = jnp.logical_not(even)
-    last, mid, mid_next, root = n - 1, n // 2, n // 2 + 1, n - 3
+    last, mid, mid_next, root = n - 1, n // 2, n // 2 + 1, n - 5
 
     def greet(target):
         pl.semaphore_signal(
@@ -66,6 +66,10 @@
     def _():
         greet(at(2))
 
+    @pl.when(me == last)
+    def _():
+        greet(last - 2)
+
     @pl.when(me == mid)
     def _():
         greet(1)
@@ -75,8 +79,9 @@
     def _():
         greet(0)
         greet(last)
-
-    @pl.when(jnp.logical_or(me < root - 2, me == last))
+        greet(last - 1)
+
+    @pl.when(jnp.logical_or(me < root - 2, me > root + 1))
     def _():
         greet(root)
 
@@ -95,6 +100,13 @@
             pl.semaphore_signal(
                 last_in, inc=1, device_id=(target,), device_id_type=pl.DeviceIdType.MESH
             )
+
+    @pl.when(me == last - 1)
+    def _():
+        pl.semaphore_wait(barrier, 4)
+        pl.semaphore_signal(
+            near_in, inc=1, device_id=(mid_next,), device_id_type=pl.DeviceIdType.MESH
+        )
 
     for load in loads:
         load.wait()
@@ -151,7 +163,11 @@
     def _():
         pl.semaphore_wait(barrier, n - 1)
 
-    @pl.when(jnp.logical_and(me != root, me != last))
+    @pl.when(me == last - 2)
+    def _():
+        pl.semaphore_wait(barrier, 4)
+
+    @pl.when(jnp.logical_and(me != root, me < last - 2))
     def _():
         pl.semaphore_wait(barrier, 3)
 
@@ -208,10 +224,17 @@
         def _():
             start(copies[slot])
 
+    direct = to_halo(own.at[1], 0, hop_send.at[0], last)
+    hop_near = to_halo(hop.at[0], 5, hop_send.at[2], last - 1)
     start_or_hop(3, 0)
     start(copies[2])
+
     start_or_hop(4, 0)
     start(copies[1])
+
+    @pl.when(me == last - 2)
+    def _():
+        start(direct)
 
     @pl.when(me == 1)
     def _():
@@ -264,13 +287,11 @@
     def _():
         start(copies[5])
 
+    def pass_right():
+        arrive(copies[2])
+        start(to_right)
+
     def left_near():
-        arrive(copies[2])
-
-        @pl.when(even)
-        def _():
-            start(to_right)
-
         arrive(copies[1])
         put_across(halo.at[2], x0.at[0, :, A])
         put_flipped(x0.at[0, :, A], x0.at[1, :, AT])
@@ -283,10 +304,11 @@
         x1[0, :, A] = new.astype(F8)
         put_flipped(x1.at[0, :, A], x1.at[1, :, AT])
 
-    def left_far():
+    def left_far(early):
         put_across(halo.at[0], spare)
         put_flipped(spare, x0.at[0, :, AT])
-        _, new = keep(square(x0[0]), x0[0, :, W])
+        inside = part_top[...] + square(x0[0, :, AT]) if early else square(x0[0])
+        _, new = keep(inside, x0[0, :, W])
         x1[0, :, W] = new.astype(F8)
         _, new = keep(between(x1, 0), x1[0, :, A])
         spare[...] = new.astype(F8)
@@ -295,7 +317,7 @@
     def right_near(split):
         arrive(copies[3])
 
-        @pl.when(odd)
+        @pl.when(jnp.logical_and(odd, me != last))
         def _():
             start(to_left)
 
@@ -319,9 +341,12 @@
         for slot in (3, 4):
             arrive(hop_in[slot])
             start(hop_out[slot])
+        pl.semaphore_wait(near_in, 1)
+        start(hop_near)
 
     @pl.when(odd)
     def _():
+        arrive(copies[2])
         left_near()
 
     @pl.when(even)
@@ -336,11 +361,20 @@
 
     @pl.when(me == last)
     def _():
+        part_top[...] = square(x0[0, :, t:])
+        part_w0[...] = square(x1[1, :, : 2 * t])
         arrive(copies[0])
-        left_far()
-        part_w0[...] = square(x1[1, :, : 2 * t])
+        left_far(True)
         part_top[...] = square(x2[0, :, AT])
         right_near(True)
+
+    @pl.when(jnp.logical_and(even, me != last - 1))
+    def _():
+        pass_right()
+
+    @pl.when(me == last - 1)
+    def _():
+        arrive(copies[2])
 
     @pl.when(even)
     def _():
@@ -369,7 +403,7 @@
             _, new = keep(first + dot_nt(x0[2, :, A], x0[3, :, W]), x0[2, :, A])
             x1[2, :, A] = new.astype(F8)
         if far:
-            left_far()
+            left_far(False)
         if not late:
             _, new = keep(square(x1[2]), x1[2, :, W])
             x2[1, :, W] = new.astype(F8)
@@ -433,17 +467,28 @@
     @pl.when(even)
     def _():
         left(copies[0])
+
+    @pl.when(jnp.logical_and(even, me != last - 1))
+    def _():
         left(to_right)
 
+    @pl.when(me == last - 2)
+    def _():
+        left(direct)
+
     @pl.when(odd)
     def _():
         left(copies[5])
+
+    @pl.when(jnp.logical_and(odd, me != last))
+    def _():
         left(to_left)
 
     @pl.when(me == mid_next)
     def _():
         left(hop_out[3])
         left(hop_out[4])
+        left(hop_near)
 
     @pl.when(me == mid)
     def _():
@@ -518,6 +563,7 @@
             pltpu.SemaphoreType.DMA,
             pltpu.SemaphoreType.REGULAR,
             pltpu.SemaphoreType.REGULAR,
+            pltpu.SemaphoreType.REGULAR,
         ],
         compiler_params=pltpu.CompilerParams(collective_id=0, has_side_effects=True, vmem_limit_bytes=32 * 2**20),
     )(truss_k, *args)

time: 21.6 us -> 21.8 us (level)
  no operation moved by 1% of the time
where the time goes in v4:
time: 21.8 us; the launch traced here: 21.6 us
  Pallas kernels  20.1 us (92%)
  between operations  1.45 us (7%)
    pallas_call x1, Pallas kernels, on_device(): pl.pallas_call(functools.partial(kernel, n), out_shape=(jax.ShapeDtypeStr...  18.3 us
    pallas_call x1, Pallas kernels, on_device(): pl.pallas_call(finish, out_shape=(jax.ShapeDtypeStruct((t, 2 * t), F32),...  1.87 us

profile of v4, /device:TPU:0, one launch (start us, length us, event | category | flops | bytes accessed | tf_op | source)
XLA Modules:
  0.0 21.6 jit_solution(10677486031062271934)
XLA Ops:
  1.3 18.3 %shard_map.68 = (f32[512,1024]{1,0:T(8,128)S(1)}, s32[32,1,128]{2,1,0:T(1,128)S(1)}) custom-call(s32[1]{0:T(128)S(6)} %copy.7.k_ref, s32[16,512]{1,0:T(8,128)} %ad_ref.1, s32[16,512]{1,0:T(8,128)} %ar_ref.1, s32[16,512]{1,0:T(8,128)} %ld_ref.1, s32[16,512]{1,0:T(8,128)} %lr_ref.1), custom_call_target="tpu_custom_call" | custom-call | tf_op jit(solution)/shard_map/pallas_call | solution.py:531
  19.5 1.9 %shard_map.69 = (f32[512,1024]{1,0:T(8,128)}, s32[3]{0:T(128)}) custom-call(f32[512,1024]{1,0:T(8,128)S(1)} %get-tuple-element.4.support_ref, s32[32,1,128]{2,1,0:T(1,128)S(1)} %get-tuple-element.5.cnt_ref), custom_call_target="tpu_custom_call" | custom-call | tf_op jit(solution)/shard_map/pallas_call | solution.py:570
